TPU v7x, 128 devices: a whole 4x4x4 slice. The times are simulated.
128 devices in a mesh: prompt: 16 (over z, x_lo, core), ctx: 8 (over x_hi, y).
Axes of the slice: x: 4 (x_hi: 2, x_lo: 2; x = x_hi * 2 + x_lo), y: 4, z: 4, core: 2. Of those that a mesh axis runs over, the one named last changes fastest.
Arguments:
- queries: bfloat16 [65536, 16, 128], P(('prompt', 'ctx')), may hold values from -8 to 8
- keys: bfloat16 [65536, 4, 128], P(('prompt', 'ctx')), may hold values from -8 to 8
- values: bfloat16 [65536, 4, 128], P(('prompt', 'ctx')), may hold values from -6 to 6
- spans: int32 [16, 2], P('prompt'), may hold values from 1 to 3072, as said below
- partner: int32 [16], replicated, may hold values from 0 to 15, each once
Outputs:
- attended: bfloat16 [65536, 16, 128], P(('prompt', 'ctx'))
- decode_cache: bfloat16 [16, 2, 16, 8, 128, 128], P('ctx', None, 'prompt')
Inputs may be any that keep to these rules, and one draw needn't show every extreme that they name: `spans`: column 0 counts the image tokens of a prompt, from 1024 to 2048, which come first; column 1 counts the text tokens after them, 1 or more; the two sum to at most 4096, and to exactly 4096 for at least one prompt.
All inputs are finite; a program needn't handle non-finite values.
Results may differ from a plain program's by a relative error of at most 0.0041.
Values may be sent and summed in bfloat16 or wider, within the bound.
A program may use at most 64 MiB of HBM per device.

v0:
```python
import math
import jax
import jax.numpy as jnp
from jax import lax
from jax.sharding import PartitionSpec as P

far_below = -1e30


def sent_together(arrays, axis, split_dim, concat_dim, along):
    widths = [a.shape[along] for a in arrays]
    both = jnp.concatenate(arrays, axis=along)
    whole = lax.all_to_all(both, axis, split_axis=split_dim, concat_axis=concat_dim, tiled=True)
    return tuple(jnp.split(whole, [sum(widths[:k]) for k in range(1, len(widths))], axis=along))


def start_state(query):
    lead_shape = query.shape[:3]
    return (
        jnp.full(lead_shape, far_below, jnp.float32),
        jnp.zeros(lead_shape, jnp.float32),
        jnp.zeros(query.shape, jnp.float32),
    )


def key_block(progress, query, query_pos, block_keys, block_values, key_first, length):
    running_peak, row_total, accumulated = progress
    score_scale = 1.0 / math.sqrt(query.shape[-1])
    scores = (
        jnp.einsum("qgmd,kgd->qgmk", query, block_keys, preferred_element_type=jnp.float32)
        * score_scale
    )
    key_pos = key_first + lax.iota(jnp.int32, block_keys.shape[0])
    allowed = ((key_pos[None, :] <= query_pos[:, None]) & (key_pos[None, :] < length))[
        :, None, None, :
    ]
    scores = jnp.where(allowed, scores, far_below)
    new_peak = jnp.maximum(running_peak, jnp.max(scores, axis=-1))
    weights = jnp.where(allowed, jnp.exp(scores - new_peak[..., None]), 0.0)
    factor = jnp.exp(running_peak - new_peak)
    row_total = row_total * factor + jnp.sum(weights, axis=-1)
    accumulated = accumulated * factor[..., None] + jnp.einsum(
        "qgmk,kgd->qgmd",
        weights.astype(jnp.bfloat16),
        block_values,
        preferred_element_type=jnp.float32,
    )
    return (new_peak, row_total, accumulated)


def fold_keys(
    progress, query, query_pos, query_last, all_keys, all_values, key_start, length, limit
):
    key_step = math.gcd(all_keys.shape[0], limit)
    block_count = all_keys.shape[0] // key_step
    key_blocks = all_keys.reshape(block_count, key_step, all_keys.shape[1], all_keys.shape[2])
    value_blocks = all_values.reshape(
        block_count, key_step, all_values.shape[1], all_values.shape[2]
    )

    def visit_block(carried, block_item):
        block_keys, block_values, block_index = block_item
        key_first = key_start + block_index * key_step
        needed = (key_first < length) & (key_first <= query_last)
        carried = lax.cond(
            needed,
            lambda held: key_block(
                held, query, query_pos, block_keys, block_values, key_first, length
            ),
            lambda held: held,
            carried,
        )
        return (carried, None)

    progress, ignored = lax.scan(
        visit_block, progress, (key_blocks, value_blocks, jnp.arange(block_count, dtype=jnp.int32))
    )
    return progress


def finish(progress, query_pos, length):
    running_peak, row_total, accumulated = progress
    mixture = accumulated / row_total[..., None]
    mixture = jnp.where((query_pos < length)[:, None, None, None], mixture, 0.0)
    return mixture.reshape(
        mixture.shape[0], mixture.shape[1] * mixture.shape[2], mixture.shape[3]
    ).astype(jnp.bfloat16)


def per_device(queries, keys, values, spans, partner):
    tok_rows, head_count, head_width = queries.shape
    kv_heads = keys.shape[1]
    blocks = lax.axis_size("ctx")
    ctx_index = lax.axis_index("ctx")
    length = spans[0, 0] + spans[0, 1]
    stripes = lax.axis_size("prompt") // kv_heads
    live_rows = (ctx_index * tok_rows + lax.iota(jnp.int32, tok_rows) < length)[:, None, None]
    handoff = jnp.stack(
        [
            jnp.where(live_rows, keys, jnp.zeros_like(keys)),
            jnp.where(live_rows, values, jnp.zeros_like(values)),
        ]
    )
    handoff = handoff.reshape(1, 2, tok_rows // stripes, stripes * kv_heads, head_width)
    handoff = lax.all_to_all(handoff, "prompt", split_axis=3, concat_axis=0, tiled=True)
    handoff = jnp.take(handoff, partner, axis=0)
    handoff = handoff.reshape(handoff.shape[0], 2, 1, 1, tok_rows // stripes, head_width)
    handoff = lax.all_to_all(handoff, "ctx", split_axis=0, concat_axis=3, tiled=True)
    head_share = head_count // blocks
    copies = max(1, blocks // kv_heads)
    own_kv = kv_heads * copies // blocks
    query_split = queries.reshape(tok_rows, blocks, head_share, head_width)
    key_split = jnp.repeat(keys, copies, axis=1).reshape(tok_rows, blocks, own_kv, head_width)
    value_split = jnp.repeat(values, copies, axis=1).reshape(tok_rows, blocks, own_kv, head_width)
    query_all, key_all, value_all = sent_together(
        (query_split, key_split, value_split), "ctx", 1, 0, 2
    )
    sequence = blocks * tok_rows
    key_all = key_all.reshape(sequence, own_kv, head_width)
    value_all = value_all.reshape(sequence, own_kv, head_width)
    query_block = math.gcd(sequence, 2048)
    block_count = sequence // query_block
    query_blocks = query_all.reshape(
        block_count, query_block, own_kv, head_share // own_kv, head_width
    )

    def one_block(block_item):
        query_part, block_index = block_item
        query_pos = block_index * query_block + lax.iota(jnp.int32, query_block)
        query_last = block_index * query_block + query_block - 1
        progress = fold_keys(
            start_state(query_part),
            query_part,
            query_pos,
            query_last,
            key_all,
            value_all,
            0,
            length,
            1024,
        )
        return finish(progress, query_pos, length)

    finished = lax.map(one_block, (query_blocks, jnp.arange(block_count, dtype=jnp.int32)))
    finished = finished.reshape(blocks, tok_rows, head_share, head_width)
    attended = lax.all_to_all(finished, "ctx", split_axis=0, concat_axis=2, tiled=True).reshape(
        tok_rows, head_count, head_width
    )
    return (attended, handoff)


def solution(mesh):
    placed = (
        P(("prompt", "ctx"), None, None),
        P(("prompt", "ctx"), None, None),
        P(("prompt", "ctx"), None, None),
        P("prompt", None),
        P(),
    )
    return jax.shard_map(
        per_device,
        mesh=mesh,
        in_specs=placed,
        out_specs=(P(("prompt", "ctx"), None, None), P("ctx", None, "prompt", None, None, None)),
        check_vma=False,
    )
```

profile of v0, /device:TPU:32, one launch (start us, length us, event | category | flops | bytes accessed | tf_op | source)
XLA Modules:
  0.0 266.5 jit_solution(13143654870239620445)
XLA Ops:
  7.9 6.4 %all-to-all-start.2 = ((bf16[1,2,128,16,128]{4,2,1,0,3:T(8,128)(2,1)}), bf16[1,2,128,16,128]{4,2,1,0,3:T(8,128)(2,1)S(1)}, u32[]{:S(2)}, u32[]{:S(2)}) async-start(bf16[1,2,128,16,128]{4,2,1,0,3:T(8,128)(2,1)} %copy.43), calls=%async_computation.2 | async-start | bytes 2097152 | tf_op jit(solution)/shard_map/all_to_all | solution.py:105
  19.1 9.1 %all-to-all-done.2 = bf16[1,2,128,16,128]{4,2,1,0,3:T(8,128)(2,1)S(1)} async-done(((bf16[1,2,128,16,128]{4,2,1,0,3:T(8,128)(2,1)}), bf16[1,2,128,16,128]{4,2,1,0,3:T(8,128)(2,1)S(1)}, u32[]{:S(2)}, u32[]{:S(2)}) %all-to-all-start.2) | async-done | bytes 1048608 | tf_op jit(solution)/shard_map/all_to_all | solution.py:105
  28.2 6.6 %all-to-all-start = ((bf16[512,8,4,128]{3,0,2,1:T(8,128)(2,1)}), bf16[512,8,4,128]{3,0,2,1:T(8,128)(2,1)}, u32[]{:S(2)}, u32[]{:S(2)}) async-start(bf16[512,8,4,128]{3,0,2,1:T(8,128)(2,1)} %pad_maximum_fusion), calls=%async_computation | async-start | bytes 8388608 | tf_op jit(solution)/shard_map/all_to_all | solution.py:13
  36.8 47.2 %all-to-all-done = bf16[512,8,4,128]{3,0,2,1:T(8,128)(2,1)} async-done(((bf16[512,8,4,128]{3,0,2,1:T(8,128)(2,1)}), bf16[512,8,4,128]{3,0,2,1:T(8,128)(2,1)}, u32[]{:S(2)}, u32[]{:S(2)}) %all-to-all-start) | async-done | bytes 4194336 | tf_op jit(solution)/shard_map/all_to_all | solution.py:13
  84.0 4.8 %all-to-all-start.3 = ((bf16[16,2,1,1,128,128]{5,4,1,3,2,0:T(8,128)(2,1)}), bf16[16,2,1,1,128,128]{5,4,1,3,2,0:T(8,128)(2,1)}, u32[]{:S(2)}, u32[]{:S(2)}) async-start(bf16[16,2,1,1,128,128]{5,4,1,3,2,0:T(8,128)(2,1)} %fusion.28), calls=%async_computation.3 | async-start | bytes 2097152 | tf_op jit(solution)/shard_map/all_to_all | solution.py:108
  94.2 133.3 %while.54 = (s32[]{:T(128)}, bf16[2,2048,2,128]{3,1,0,2:T(8,128)(2,1)}, s32[2]{0:T(128)S(1)}, s32[]{:T(128)}, bf16[4096,1,1,128]{3,0,2,1:T(8,128)(2,1)}, /*index...) while((s32[]{:T(128)}, ...), condition=%wide.region_7.8_spmd, body=%wide.region_0.7_spmd.sunk | while | flops 2208846848 | bytes 78479512 | solution.py:144
  99.4 41.4 %while.55 = (s32[]{:T(128)}, f32[2048,1,2]{0,2,1:T(2,128)S(1)}, f32[2048,1,2]{0,2,1:T(2,128)S(1)}, f32[2048,1,2,128]{0,3,2,1:T(8,128)S(1)}, s32[4]{0:T(128)S(1)}...) while((s32[]{:T(128)}, f32[2048,1,2]{0,2,1:T(2,128)S(1)}, ...), condition=%wide.region_6.6_spmd.clone, body=%wide.region_1.5_spmd.clone.sunk | while | flops 2207269888 | bytes 64793936 | solution.py:75
  100.7 18.1 %conditional.3 = ((f32[2048,1,2]{0,2,1:T(2,128)S(1)}, f32[2048,1,2]{0,2,1:T(2,128)S(1)}, f32[2048,1,2,128]{0,3,2,1:T(8,128)S(1)})) conditional(s32[]{:T(128)} %convert_element_type.42, (f32[2048,1,2]{0,2,1:T(2,128)S(1)}, f32[2048,1,2]{0,2,1:T(2,128)S(1)}, f32[2048,1,2,128]{0,3,2,1:T(8,128)S(1)}) %tuple.87, (s32[]{:T(128)}, s32[]{:T(128)}, s32[]{:T(128)}, ...), branch_computations={%region_2.1_spmd, %region_3.4_spmd} | conditional | flops 2207269888 | bytes 64785456 | solution.py:65
  102.5 4.6 %fusion.2 = (f32[2048,2]{0,1:T(2,128)S(1)}, f32[1024,2048,2]{1,0,2:T(8,128)S(1)}) fusion(pred[2048,1024]{0,1:T(8,128)(4,1)S(1)} %compare_and_fusion, bf16[2048,1,2,128]{3,0,2,1:T(8,128)(2,1)S(1)} %get-tuple-element.259, bf16[4,1024,1,128]{3,1,2,0:T(8,128)(2,1)} %get-tuple-element.257, s32[]{:T(128)} %get-tuple-element.258), kind=kOutput, calls=%fused_computation.4 | convolution fusion | flops 1086320640 | bytes 20201984 | tf_op jit(solution)/shard_map/while/body/eval_jaxpr/while/body/eval_jaxpr/cond/branch_1_fun/qgmd,kgd->qgmk/dot_general | solution.py:30
  107.1 7.1 %fusion.12 = f32[2048,1,2,128]{0,3,2,1:T(8,128)S(1)} fusion(f32[1024,2048,2]{1,0,2:T(8,128)S(1)} %get-tuple-element.429, f32[2048,2]{0,1:T(2,128)S(1)} %bitcast.119, pred[2048,1024]{0,1:T(8,128)(4,1)S(1)} %compare_and_fusion, f32[2048,1,2,128]{0,3,2,1:T(8,128)S(1)} %get-tuple-element.261, f32[2048,2]{0,1:T(2,128)S(1)} %get-tuple-element.426, ...), kind=kOutput, calls=%fused_computation.12 | convolution fusion | flops 1095761920 | bytes 23364096 | tf_op jit(solution)/shard_map/while/body/eval_jaxpr/while/body/eval_jaxpr/cond/branch_1_fun/qgmk,kgd->qgmd/dot_general | solution.py:42
  120.1 18.1 %conditional.3 = ((f32[2048,1,2]{0,2,1:T(2,128)S(1)}, f32[2048,1,2]{0,2,1:T(2,128)S(1)}, f32[2048,1,2,128]{0,3,2,1:T(8,128)S(1)})) conditional(s32[]{:T(128)} %convert_element_type.42, (f32[2048,1,2]{0,2,1:T(2,128)S(1)}, f32[2048,1,2]{0,2,1:T(2,128)S(1)}, f32[2048,1,2,128]{0,3,2,1:T(8,128)S(1)}) %tuple.87, (s32[]{:T(128)}, s32[]{:T(128)}, s32[]{:T(128)}, ...), branch_computations={%region_2.1_spmd, %region_3.4_spmd} | conditional | flops 2207269888 | bytes 64785456 | solution.py:65
  126.5 7.1 %fusion.12 = f32[2048,1,2,128]{0,3,2,1:T(8,128)S(1)} fusion(f32[1024,2048,2]{1,0,2:T(8,128)S(1)} %get-tuple-element.429, f32[2048,2]{0,1:T(2,128)S(1)} %bitcast.119, pred[2048,1024]{0,1:T(8,128)(4,1)S(1)} %compare_and_fusion, f32[2048,1,2,128]{0,3,2,1:T(8,128)S(1)} %get-tuple-element.261, f32[2048,2]{0,1:T(2,128)S(1)} %get-tuple-element.426, ...), kind=kOutput, calls=%fused_computation.12 | convolution fusion | flops 1095761920 | bytes 23364096 | tf_op jit(solution)/shard_map/while/body/eval_jaxpr/while/body/eval_jaxpr/cond/branch_1_fun/qgmk,kgd->qgmd/dot_general | solution.py:42
  148.0 77.5 %while.55 = (s32[]{:T(128)}, f32[2048,1,2]{0,2,1:T(2,128)S(1)}, f32[2048,1,2]{0,2,1:T(2,128)S(1)}, f32[2048,1,2,128]{0,3,2,1:T(8,128)S(1)}, s32[4]{0:T(128)S(1)}...) while((s32[]{:T(128)}, f32[2048,1,2]{0,2,1:T(2,128)S(1)}, ...), condition=%wide.region_6.6_spmd.clone, body=%wide.region_1.5_spmd.clone.sunk | while | flops 2207269888 | bytes 64793936 | solution.py:75
  149.3 18.0 %conditional.3 = ((f32[2048,1,2]{0,2,1:T(2,128)S(1)}, f32[2048,1,2]{0,2,1:T(2,128)S(1)}, f32[2048,1,2,128]{0,3,2,1:T(8,128)S(1)})) conditional(s32[]{:T(128)} %convert_element_type.42, (f32[2048,1,2]{0,2,1:T(2,128)S(1)}, f32[2048,1,2]{0,2,1:T(2,128)S(1)}, f32[2048,1,2,128]{0,3,2,1:T(8,128)S(1)}) %tuple.87, (s32[]{:T(128)}, s32[]{:T(128)}, s32[]{:T(128)}, ...), branch_computations={%region_2.1_spmd, %region_3.4_spmd} | conditional | flops 2207269888 | bytes 64785456 | solution.py:65
  155.7 7.1 %fusion.12 = f32[2048,1,2,128]{0,3,2,1:T(8,128)S(1)} fusion(f32[1024,2048,2]{1,0,2:T(8,128)S(1)} %get-tuple-element.429, f32[2048,2]{0,1:T(2,128)S(1)} %bitcast.119, pred[2048,1024]{0,1:T(8,128)(4,1)S(1)} %compare_and_fusion, f32[2048,1,2,128]{0,3,2,1:T(8,128)S(1)} %get-tuple-element.261, f32[2048,2]{0,1:T(2,128)S(1)} %get-tuple-element.426, ...), kind=kOutput, calls=%fused_computation.12 | convolution fusion | flops 1095761920 | bytes 23364096 | tf_op jit(solution)/shard_map/while/body/eval_jaxpr/while/body/eval_jaxpr/cond/branch_1_fun/qgmk,kgd->qgmd/dot_general | solution.py:42
  168.6 18.1 %conditional.3 = ((f32[2048,1,2]{0,2,1:T(2,128)S(1)}, f32[2048,1,2]{0,2,1:T(2,128)S(1)}, f32[2048,1,2,128]{0,3,2,1:T(8,128)S(1)})) conditional(s32[]{:T(128)} %convert_element_type.42, (f32[2048,1,2]{0,2,1:T(2,128)S(1)}, f32[2048,1,2]{0,2,1:T(2,128)S(1)}, f32[2048,1,2,128]{0,3,2,1:T(8,128)S(1)}) %tuple.87, (s32[]{:T(128)}, s32[]{:T(128)}, s32[]{:T(128)}, ...), branch_computations={%region_2.1_spmd, %region_3.4_spmd} | conditional | flops 2207269888 | bytes 64785456 | solution.py:65
  170.4 4.6 %fusion.2 = (f32[2048,2]{0,1:T(2,128)S(1)}, f32[1024,2048,2]{1,0,2:T(8,128)S(1)}) fusion(pred[2048,1024]{0,1:T(8,128)(4,1)S(1)} %compare_and_fusion, bf16[2048,1,2,128]{3,0,2,1:T(8,128)(2,1)S(1)} %get-tuple-element.259, bf16[4,1024,1,128]{3,1,2,0:T(8,128)(2,1)} %get-tuple-element.257, s32[]{:T(128)} %get-tuple-element.258), kind=kOutput, calls=%fused_computation.4 | convolution fusion | flops 1086320640 | bytes 20201984 | tf_op jit(solution)/shard_map/while/body/eval_jaxpr/while/body/eval_jaxpr/cond/branch_1_fun/qgmd,kgd->qgmk/dot_general | solution.py:30
  175.1 7.1 %fusion.12 = f32[2048,1,2,128]{0,3,2,1:T(8,128)S(1)} fusion(f32[1024,2048,2]{1,0,2:T(8,128)S(1)} %get-tuple-element.429, f32[2048,2]{0,1:T(2,128)S(1)} %bitcast.119, pred[2048,1024]{0,1:T(8,128)(4,1)S(1)} %compare_and_fusion, f32[2048,1,2,128]{0,3,2,1:T(8,128)S(1)} %get-tuple-element.261, f32[2048,2]{0,1:T(2,128)S(1)} %get-tuple-element.426, ...), kind=kOutput, calls=%fused_computation.12 | convolution fusion | flops 1095761920 | bytes 23364096 | tf_op jit(solution)/shard_map/while/body/eval_jaxpr/while/body/eval_jaxpr/cond/branch_1_fun/qgmk,kgd->qgmd/dot_general | solution.py:42
  188.0 18.1 %conditional.3 = ((f32[2048,1,2]{0,2,1:T(2,128)S(1)}, f32[2048,1,2]{0,2,1:T(2,128)S(1)}, f32[2048,1,2,128]{0,3,2,1:T(8,128)S(1)})) conditional(s32[]{:T(128)} %convert_element_type.42, (f32[2048,1,2]{0,2,1:T(2,128)S(1)}, f32[2048,1,2]{0,2,1:T(2,128)S(1)}, f32[2048,1,2,128]{0,3,2,1:T(8,128)S(1)}) %tuple.87, (s32[]{:T(128)}, s32[]{:T(128)}, s32[]{:T(128)}, ...), branch_computations={%region_2.1_spmd, %region_3.4_spmd} | conditional | flops 2207269888 | bytes 64785456 | solution.py:65
  194.4 7.1 %fusion.12 = f32[2048,1,2,128]{0,3,2,1:T(8,128)S(1)} fusion(f32[1024,2048,2]{1,0,2:T(8,128)S(1)} %get-tuple-element.429, f32[2048,2]{0,1:T(2,128)S(1)} %bitcast.119, pred[2048,1024]{0,1:T(8,128)(4,1)S(1)} %compare_and_fusion, f32[2048,1,2,128]{0,3,2,1:T(8,128)S(1)} %get-tuple-element.261, f32[2048,2]{0,1:T(2,128)S(1)} %get-tuple-element.426, ...), kind=kOutput, calls=%fused_computation.12 | convolution fusion | flops 1095761920 | bytes 23364096 | tf_op jit(solution)/shard_map/while/body/eval_jaxpr/while/body/eval_jaxpr/cond/branch_1_fun/qgmk,kgd->qgmd/dot_general | solution.py:42
  207.4 18.1 %conditional.3 = ((f32[2048,1,2]{0,2,1:T(2,128)S(1)}, f32[2048,1,2]{0,2,1:T(2,128)S(1)}, f32[2048,1,2,128]{0,3,2,1:T(8,128)S(1)})) conditional(s32[]{:T(128)} %convert_element_type.42, (f32[2048,1,2]{0,2,1:T(2,128)S(1)}, f32[2048,1,2]{0,2,1:T(2,128)S(1)}, f32[2048,1,2,128]{0,3,2,1:T(8,128)S(1)}) %tuple.87, (s32[]{:T(128)}, s32[]{:T(128)}, s32[]{:T(128)}, ...), branch_computations={%region_2.1_spmd, %region_3.4_spmd} | conditional | flops 2207269888 | bytes 64785456 | solution.py:65
  213.8 7.1 %fusion.12 = f32[2048,1,2,128]{0,3,2,1:T(8,128)S(1)} fusion(f32[1024,2048,2]{1,0,2:T(8,128)S(1)} %get-tuple-element.429, f32[2048,2]{0,1:T(2,128)S(1)} %bitcast.119, pred[2048,1024]{0,1:T(8,128)(4,1)S(1)} %compare_and_fusion, f32[2048,1,2,128]{0,3,2,1:T(8,128)S(1)} %get-tuple-element.261, f32[2048,2]{0,1:T(2,128)S(1)} %get-tuple-element.426, ...), kind=kOutput, calls=%fused_computation.12 | convolution fusion | flops 1095761920 | bytes 23364096 | tf_op jit(solution)/shard_map/while/body/eval_jaxpr/while/body/eval_jaxpr/cond/branch_1_fun/qgmk,kgd->qgmd/dot_general | solution.py:42
  230.6 7.2 %all-to-all-start.1 = ((bf16[8,512,2,128]{3,1,2,0:T(8,128)(2,1)}), bf16[8,512,2,128]{3,1,2,0:T(8,128)(2,1)S(1)}, u32[]{:S(2)}, u32[]{:S(2)}) async-start(bf16[8,512,2,128]{3,1,2,0:T(8,128)(2,1)} %copy.42), calls=%async_computation.1 | async-start | bytes 4194304 | tf_op jit(solution)/shard_map/all_to_all | solution.py:146
  240.1 23.7 %all-to-all-done.1 = bf16[8,512,2,128]{3,1,2,0:T(8,128)(2,1)S(1)} async-done(((bf16[8,512,2,128]{3,1,2,0:T(8,128)(2,1)}), bf16[8,512,2,128]{3,1,2,0:T(8,128)(2,1)S(1)}, u32[]{:S(2)}, u32[]{:S(2)}) %all-to-all-start.1) | async-done | bytes 2097184 | tf_op jit(solution)/shard_map/all_to_all | solution.py:146
  (123 shorter events, 100.5 us)
Async XLA Ops:
  3.3 11.0 %copy-start = (bf16[512,4,128]{2,1,0:T(4,128)(2,1)S(1)}, bf16[512,4,128]{2,1,0:T(4,128)(2,1)}, u32[]{:S(2)}) copy-start(bf16[512,4,128]{2,1,0:T(4,128)(2,1)} %param.12) | copy-start | bytes 1572868
  6.5 7.8 %copy-start.1 = (bf16[512,4,128]{2,1,0:T(4,128)(2,1)S(1)}, bf16[512,4,128]{2,1,0:T(4,128)(2,1)}, u32[]{:S(2)}) copy-start(bf16[512,4,128]{2,1,0:T(4,128)(2,1)} %param.13) | copy-start | bytes 1572868
  7.9 20.3 %all-to-all-start.2 = ((bf16[1,2,128,16,128]{4,2,1,0,3:T(8,128)(2,1)}), bf16[1,2,128,16,128]{4,2,1,0,3:T(8,128)(2,1)S(1)}, u32[]{:S(2)}, u32[]{:S(2)}) async-start(bf16[1,2,128,16,128]{4,2,1,0,3:T(8,128)(2,1)} %copy.43), calls=%async_computation.2 | async-start | bytes 2097152 | tf_op jit(solution)/shard_map/all_to_all | solution.py:105
  19.1 15.7 %copy-start.2 = (s32[16]{0:T(128)S(1)}, s32[16]{0:T(128)}, u32[]{:S(2)}) copy-start(s32[16]{0:T(128)} %param.15) | copy-start | bytes 196
  28.2 55.9 %all-to-all-start = ((bf16[512,8,4,128]{3,0,2,1:T(8,128)(2,1)}), bf16[512,8,4,128]{3,0,2,1:T(8,128)(2,1)}, u32[]{:S(2)}, u32[]{:S(2)}) async-start(bf16[512,8,4,128]{3,0,2,1:T(8,128)(2,1)} %pad_maximum_fusion), calls=%async_computation | async-start | bytes 8388608 | tf_op jit(solution)/shard_map/all_to_all | solution.py:13
  84.0 146.5 %all-to-all-start.3 = ((bf16[16,2,1,1,128,128]{5,4,1,3,2,0:T(8,128)(2,1)}), bf16[16,2,1,1,128,128]{5,4,1,3,2,0:T(8,128)(2,1)}, u32[]{:S(2)}, u32[]{:S(2)}) async-start(bf16[16,2,1,1,128,128]{5,4,1,3,2,0:T(8,128)(2,1)} %fusion.28), calls=%async_computation.3 | async-start | bytes 2097152 | tf_op jit(solution)/shard_map/all_to_all | solution.py:108
  230.6 33.2 %all-to-all-start.1 = ((bf16[8,512,2,128]{3,1,2,0:T(8,128)(2,1)}), bf16[8,512,2,128]{3,1,2,0:T(8,128)(2,1)S(1)}, u32[]{:S(2)}, u32[]{:S(2)}) async-start(bf16[8,512,2,128]{3,1,2,0:T(8,128)(2,1)} %copy.42), calls=%async_computation.1 | async-start | bytes 4194304 | tf_op jit(solution)/shard_map/all_to_all | solution.py:146
where the time goes:
time: 268 us; the launch traced here: 266 us
  waiting for transfers between devices  80 us (30%)
  matrix products  70.1 us (26%)
  other arithmetic  45.1 us (17%)
  local copies, waits for them, and re-layouts  36.9 us (14%)
  starting transfers between devices  25 us (9%)
  loops' own time  7.36 us (3%)
    all_to_all x1, waiting for transfers between devices, sent_together(): lax.all_to_all(both, axis, split_axis=split_dim, concat_axis=concat_dim,...  47.2 us
    dot_general x6, matrix products, key_block(): jnp.einsum('qgmk,kgd->qgmd', weights.astype(jnp.bfloat16), block_values,...  42.4 us
    dot_general x6, matrix products, key_block(): jnp.einsum('qgmd,kgd->qgmk', query, block_keys, preferred_element_type=jn...  27.7 us
    reduce_sum x6, other arithmetic, key_block(): row_total = row_total * factor + jnp.sum(weights, axis=-1)  27.1 us
    all_to_all x1, waiting for transfers between devices, per_device(): lax.all_to_all(finished, 'ctx', split_axis=0, concat_axis=2, tiled=True)  23.7 us
    and x6, other arithmetic, key_block(): (key_pos[None, :] <= query_pos[:, None]) & (key_pos[None, :] < length)  10.2 us
    all_to_all x1, waiting for transfers between devices, per_device(): lax.all_to_all(handoff, 'prompt', split_axis=3, concat_axis=0, tiled=True)  9.08 us
    unnamed x11, local copies, waits for them, and re-layouts  7.27 us
  transfers between devices with their start and end apart: 4, of which 3 were waited for; matrix products, arithmetic and copies ran while one was open for 54% of the time, Pallas kernels for 0%

commit v1 on v0

--- a/solution.py
+++ b/solution.py
@@ -3,6 +3,7 @@
 import jax.numpy as jnp
 from jax import lax
 from jax.sharding import PartitionSpec as P
+from jax.lax import all_to_all, axis_size
 
 far_below = -1e30
 
@@ -102,7 +103,10 @@
         ]
     )
     handoff = handoff.reshape(1, 2, tok_rows // stripes, stripes * kv_heads, head_width)
-    handoff = lax.all_to_all(handoff, "prompt", split_axis=3, concat_axis=0, tiled=True)
+    number_array = lambda load: jnp.concatenate(
+        all_to_all(jnp.stack(jnp.split(load, axis_size("prompt"), axis=3)), "prompt", 0, 0), axis=0
+    )
+    handoff = number_array(handoff)
     handoff = jnp.take(handoff, partner, axis=0)
     handoff = handoff.reshape(handoff.shape[0], 2, 1, 1, tok_rows // stripes, head_width)
     handoff = lax.all_to_all(handoff, "ctx", split_axis=0, concat_axis=3, tiled=True)

time: 268 us -> 279 us (1.041)
  local copies, waits for them, and re-layouts: 36.9 us -> 45.8 us
    unnamed x11 -> x26, local copies, waits for them, and re-layouts: 7.27 us -> 16.9 us
  transfers between devices with their start and end apart: 4 -> 4, of which waited for: 3 -> 3; matrix products, arithmetic and copies ran while one was open for 54% -> 52% of each run, Pallas kernels for 0% -> 0%
where the time goes in v1:
time: 279 us; the launch traced here: 278 us
  waiting for transfers between devices  80 us (29%)
  matrix products  70.1 us (25%)
  other arithmetic  47.7 us (17%)
  local copies, waits for them, and re-layouts  45.8 us (16%)
  starting transfers between devices  25 us (9%)
  loops' own time  7.26 us (3%)
    all_to_all x1, waiting for transfers between devices, sent_together(): lax.all_to_all(both, axis, split_axis=split_dim, concat_axis=concat_dim,...  47.2 us
    dot_general x6, matrix products, key_block(): jnp.einsum('qgmk,kgd->qgmd', weights.astype(jnp.bfloat16), block_values,...  42.4 us
    dot_general x6, matrix products, key_block(): jnp.einsum('qgmd,kgd->qgmk', query, block_keys, preferred_element_type=jn...  27.7 us
    reduce_sum x6, other arithmetic, key_block(): row_total = row_total * factor + jnp.sum(weights, axis=-1)  27.1 us
    all_to_all x1, waiting for transfers between devices, per_device(): lax.all_to_all(finished, 'ctx', split_axis=0, concat_axis=2, tiled=True)  23.7 us
    unnamed x26, local copies, waits for them, and re-layouts  16.9 us
    and x6, other arithmetic, key_block(): (key_pos[None, :] <= query_pos[:, None]) & (key_pos[None, :] < length)  10.2 us
    all_to_all x1, waiting for transfers between devices, per_device(): all_to_all(jnp.stack(jnp.split(load, axis_size('prompt'), axis=3)), 'prom...  9.07 us
  transfers between devices with their start and end apart: 4, of which 3 were waited for; matrix products, arithmetic and copies ran while one was open for 52% of the time, Pallas kernels for 0%

profile of v1, /device:TPU:32, one launch (start us, length us, event | category | flops | bytes accessed | tf_op | source)
XLA Modules:
  0.0 277.8 jit_solution(15981988160392137673)
XLA Ops:
  19.5 6.4 %all-to-all-start.2 = ((bf16[16,1,2,128,1,128]{5,3,2,4,1,0:T(8,128)(2,1)}), bf16[16,1,2,128,1,128]{5,3,2,4,1,0:T(8,128)(2,1)S(1)}, u32[]{:S(2)}, u32[]{:S(2)}) async-start(bf16[16,1,2,128,1,128]{5,3,2,4,1,0:T(8,128)(2,1)} %bitcast_dynamic-update-slice_fusion), calls=%async_computation.2 | async-start | bytes 2097152 | tf_op jit(solution)/shard_map/all_to_all | solution.py:107
  30.7 9.1 %all-to-all-done.2 = bf16[16,1,2,128,1,128]{5,3,2,4,1,0:T(8,128)(2,1)S(1)} async-done(((bf16[16,1,2,128,1,128]{5,3,2,4,1,0:T(8,128)(2,1)}), bf16[16,1,2,128,1,128]{5,3,2,4,1,0:T(8,128)(2,1)S(1)}, u32[]{:S(2)}, u32[]{:S(2)}) %all-to-all-start.2) | async-done | bytes 1048608 | tf_op jit(solution)/shard_map/all_to_all | solution.py:107
  39.8 6.6 %all-to-all-start = ((bf16[512,8,4,128]{3,0,2,1:T(8,128)(2,1)}), bf16[512,8,4,128]{3,0,2,1:T(8,128)(2,1)}, u32[]{:S(2)}, u32[]{:S(2)}) async-start(bf16[512,8,4,128]{3,0,2,1:T(8,128)(2,1)} %pad_maximum_fusion), calls=%async_computation | async-start | bytes 8388608 | tf_op jit(solution)/shard_map/all_to_all | solution.py:14
  48.4 47.2 %all-to-all-done = bf16[512,8,4,128]{3,0,2,1:T(8,128)(2,1)} async-done(((bf16[512,8,4,128]{3,0,2,1:T(8,128)(2,1)}), bf16[512,8,4,128]{3,0,2,1:T(8,128)(2,1)}, u32[]{:S(2)}, u32[]{:S(2)}) %all-to-all-start) | async-done | bytes 4194336 | tf_op jit(solution)/shard_map/all_to_all | solution.py:14
  95.6 4.8 %all-to-all-start.3 = ((bf16[16,2,1,1,128,128]{5,4,1,3,2,0:T(8,128)(2,1)}), bf16[16,2,1,1,128,128]{5,4,1,3,2,0:T(8,128)(2,1)}, u32[]{:S(2)}, u32[]{:S(2)}) async-start(bf16[16,2,1,1,128,128]{5,4,1,3,2,0:T(8,128)(2,1)} %fusion.28), calls=%async_computation.3 | async-start | bytes 2097152 | tf_op jit(solution)/shard_map/all_to_all | solution.py:112
  105.8 133.0 %while.54 = (s32[]{:T(128)}, bf16[2,2048,2,128]{3,1,0,2:T(8,128)(2,1)}, s32[2]{0:T(128)S(1)}, s32[]{:T(128)}, bf16[4096,1,1,128]{3,0,2,1:T(8,128)(2,1)}, /*index...) while((s32[]{:T(128)}, ...), condition=%wide.region_7.8_spmd, body=%wide.region_0.7_spmd.sunk | while | flops 2208846848 | bytes 78479024 | solution.py:148
  110.8 41.4 %while.55 = (s32[]{:T(128)}, f32[2048,1,2]{0,2,1:T(2,128)S(1)}, f32[2048,1,2]{0,2,1:T(2,128)S(1)}, f32[2048,1,2,128]{0,3,2,1:T(8,128)S(1)}, s32[4]{0:T(128)S(1)}...) while((s32[]{:T(128)}, f32[2048,1,2]{0,2,1:T(2,128)S(1)}, ...), condition=%wide.region_6.6_spmd.clone, body=%wide.region_1.5_spmd.clone.sunk | while | flops 2207269888 | bytes 64793944 | solution.py:76
  112.2 18.1 %conditional.3 = ((f32[2048,1,2]{0,2,1:T(2,128)S(1)}, f32[2048,1,2]{0,2,1:T(2,128)S(1)}, f32[2048,1,2,128]{0,3,2,1:T(8,128)S(1)})) conditional(s32[]{:T(128)} %convert_element_type.42, (f32[2048,1,2]{0,2,1:T(2,128)S(1)}, f32[2048,1,2]{0,2,1:T(2,128)S(1)}, f32[2048,1,2,128]{0,3,2,1:T(8,128)S(1)}) %tuple.146, (s32[]{:T(128)}, s32[]{:T(128)}, s32[]{:T(128)}, ...), branch_computations={%region_2.1_spmd, %region_3.4_spmd} | conditional | flops 2207269888 | bytes 64785456 | solution.py:66
  123.1 7.1 %fusion.12 = f32[2048,1,2,128]{0,3,2,1:T(8,128)S(1)} fusion(f32[1024,2048,2]{1,0,2:T(8,128)S(1)} %get-tuple-element.729, f32[2048,2]{0,1:T(2,128)S(1)} %bitcast.148, pred[2048,1024]{0,1:T(8,128)(4,1)S(1)} %compare_and_fusion, f32[2048,1,2,128]{0,3,2,1:T(8,128)S(1)} %get-tuple-element.261, f32[2048,2]{0,1:T(2,128)S(1)} %get-tuple-element.726, ...), kind=kOutput, calls=%fused_computation.12 | convolution fusion | flops 1095761920 | bytes 23364096 | tf_op jit(solution)/shard_map/while/body/eval_jaxpr/while/body/eval_jaxpr/cond/branch_1_fun/qgmk,kgd->qgmd/dot_general | solution.py:43
  131.5 18.0 %conditional.3 = ((f32[2048,1,2]{0,2,1:T(2,128)S(1)}, f32[2048,1,2]{0,2,1:T(2,128)S(1)}, f32[2048,1,2,128]{0,3,2,1:T(8,128)S(1)})) conditional(s32[]{:T(128)} %convert_element_type.42, (f32[2048,1,2]{0,2,1:T(2,128)S(1)}, f32[2048,1,2]{0,2,1:T(2,128)S(1)}, f32[2048,1,2,128]{0,3,2,1:T(8,128)S(1)}) %tuple.146, (s32[]{:T(128)}, s32[]{:T(128)}, s32[]{:T(128)}, ...), branch_computations={%region_2.1_spmd, %region_3.4_spmd} | conditional | flops 2207269888 | bytes 64785456 | solution.py:66
  133.3 4.6 %fusion.2 = (f32[2048,2]{0,1:T(2,128)S(1)}, f32[1024,2048,2]{1,0,2:T(8,128)S(1)}) fusion(pred[2048,1024]{0,1:T(8,128)(4,1)S(1)} %compare_and_fusion, bf16[2048,1,2,128]{3,0,2,1:T(8,128)(2,1)S(1)} %get-tuple-element.259, bf16[4,1024,1,128]{3,1,2,0:T(8,128)(2,1)} %get-tuple-element.257, s32[]{:T(128)} %get-tuple-element.258), kind=kOutput, calls=%fused_computation.4 | convolution fusion | flops 1086320640 | bytes 20201984 | tf_op jit(solution)/shard_map/while/body/eval_jaxpr/while/body/eval_jaxpr/cond/branch_1_fun/qgmd,kgd->qgmk/dot_general | solution.py:31
  142.5 7.1 %fusion.12 = f32[2048,1,2,128]{0,3,2,1:T(8,128)S(1)} fusion(f32[1024,2048,2]{1,0,2:T(8,128)S(1)} %get-tuple-element.729, f32[2048,2]{0,1:T(2,128)S(1)} %bitcast.148, pred[2048,1024]{0,1:T(8,128)(4,1)S(1)} %compare_and_fusion, f32[2048,1,2,128]{0,3,2,1:T(8,128)S(1)} %get-tuple-element.261, f32[2048,2]{0,1:T(2,128)S(1)} %get-tuple-element.726, ...), kind=kOutput, calls=%fused_computation.12 | convolution fusion | flops 1095761920 | bytes 23364096 | tf_op jit(solution)/shard_map/while/body/eval_jaxpr/while/body/eval_jaxpr/cond/branch_1_fun/qgmk,kgd->qgmd/dot_general | solution.py:43
  159.3 77.5 %while.55 = (s32[]{:T(128)}, f32[2048,1,2]{0,2,1:T(2,128)S(1)}, f32[2048,1,2]{0,2,1:T(2,128)S(1)}, f32[2048,1,2,128]{0,3,2,1:T(8,128)S(1)}, s32[4]{0:T(128)S(1)}...) while((s32[]{:T(128)}, f32[2048,1,2]{0,2,1:T(2,128)S(1)}, ...), condition=%wide.region_6.6_spmd.clone, body=%wide.region_1.5_spmd.clone.sunk | while | flops 2207269888 | bytes 64793944 | solution.py:76
  160.6 18.0 %conditional.3 = ((f32[2048,1,2]{0,2,1:T(2,128)S(1)}, f32[2048,1,2]{0,2,1:T(2,128)S(1)}, f32[2048,1,2,128]{0,3,2,1:T(8,128)S(1)})) conditional(s32[]{:T(128)} %convert_element_type.42, (f32[2048,1,2]{0,2,1:T(2,128)S(1)}, f32[2048,1,2]{0,2,1:T(2,128)S(1)}, f32[2048,1,2,128]{0,3,2,1:T(8,128)S(1)}) %tuple.146, (s32[]{:T(128)}, s32[]{:T(128)}, s32[]{:T(128)}, ...), branch_computations={%region_2.1_spmd, %region_3.4_spmd} | conditional | flops 2207269888 | bytes 64785456 | solution.py:66
  171.6 7.1 %fusion.12 = f32[2048,1,2,128]{0,3,2,1:T(8,128)S(1)} fusion(f32[1024,2048,2]{1,0,2:T(8,128)S(1)} %get-tuple-element.729, f32[2048,2]{0,1:T(2,128)S(1)} %bitcast.148, pred[2048,1024]{0,1:T(8,128)(4,1)S(1)} %compare_and_fusion, f32[2048,1,2,128]{0,3,2,1:T(8,128)S(1)} %get-tuple-element.261, f32[2048,2]{0,1:T(2,128)S(1)} %get-tuple-element.726, ...), kind=kOutput, calls=%fused_computation.12 | convolution fusion | flops 1095761920 | bytes 23364096 | tf_op jit(solution)/shard_map/while/body/eval_jaxpr/while/body/eval_jaxpr/cond/branch_1_fun/qgmk,kgd->qgmd/dot_general | solution.py:43
  180.0 18.0 %conditional.3 = ((f32[2048,1,2]{0,2,1:T(2,128)S(1)}, f32[2048,1,2]{0,2,1:T(2,128)S(1)}, f32[2048,1,2,128]{0,3,2,1:T(8,128)S(1)})) conditional(s32[]{:T(128)} %convert_element_type.42, (f32[2048,1,2]{0,2,1:T(2,128)S(1)}, f32[2048,1,2]{0,2,1:T(2,128)S(1)}, f32[2048,1,2,128]{0,3,2,1:T(8,128)S(1)}) %tuple.146, (s32[]{:T(128)}, s32[]{:T(128)}, s32[]{:T(128)}, ...), branch_computations={%region_2.1_spmd, %region_3.4_spmd} | conditional | flops 2207269888 | bytes 64785456 | solution.py:66
  181.8 4.6 %fusion.2 = (f32[2048,2]{0,1:T(2,128)S(1)}, f32[1024,2048,2]{1,0,2:T(8,128)S(1)}) fusion(pred[2048,1024]{0,1:T(8,128)(4,1)S(1)} %compare_and_fusion, bf16[2048,1,2,128]{3,0,2,1:T(8,128)(2,1)S(1)} %get-tuple-element.259, bf16[4,1024,1,128]{3,1,2,0:T(8,128)(2,1)} %get-tuple-element.257, s32[]{:T(128)} %get-tuple-element.258), kind=kOutput, calls=%fused_computation.4 | convolution fusion | flops 1086320640 | bytes 20201984 | tf_op jit(solution)/shard_map/while/body/eval_jaxpr/while/body/eval_jaxpr/cond/branch_1_fun/qgmd,kgd->qgmk/dot_general | solution.py:31
  191.0 7.1 %fusion.12 = f32[2048,1,2,128]{0,3,2,1:T(8,128)S(1)} fusion(f32[1024,2048,2]{1,0,2:T(8,128)S(1)} %get-tuple-element.729, f32[2048,2]{0,1:T(2,128)S(1)} %bitcast.148, pred[2048,1024]{0,1:T(8,128)(4,1)S(1)} %compare_and_fusion, f32[2048,1,2,128]{0,3,2,1:T(8,128)S(1)} %get-tuple-element.261, f32[2048,2]{0,1:T(2,128)S(1)} %get-tuple-element.726, ...), kind=kOutput, calls=%fused_computation.12 | convolution fusion | flops 1095761920 | bytes 23364096 | tf_op jit(solution)/shard_map/while/body/eval_jaxpr/while/body/eval_jaxpr/cond/branch_1_fun/qgmk,kgd->qgmd/dot_general | solution.py:43
  199.4 18.0 %conditional.3 = ((f32[2048,1,2]{0,2,1:T(2,128)S(1)}, f32[2048,1,2]{0,2,1:T(2,128)S(1)}, f32[2048,1,2,128]{0,3,2,1:T(8,128)S(1)})) conditional(s32[]{:T(128)} %convert_element_type.42, (f32[2048,1,2]{0,2,1:T(2,128)S(1)}, f32[2048,1,2]{0,2,1:T(2,128)S(1)}, f32[2048,1,2,128]{0,3,2,1:T(8,128)S(1)}) %tuple.146, (s32[]{:T(128)}, s32[]{:T(128)}, s32[]{:T(128)}, ...), branch_computations={%region_2.1_spmd, %region_3.4_spmd} | conditional | flops 2207269888 | bytes 64785456 | solution.py:66
  210.3 7.1 %fusion.12 = f32[2048,1,2,128]{0,3,2,1:T(8,128)S(1)} fusion(f32[1024,2048,2]{1,0,2:T(8,128)S(1)} %get-tuple-element.729, f32[2048,2]{0,1:T(2,128)S(1)} %bitcast.148, pred[2048,1024]{0,1:T(8,128)(4,1)S(1)} %compare_and_fusion, f32[2048,1,2,128]{0,3,2,1:T(8,128)S(1)} %get-tuple-element.261, f32[2048,2]{0,1:T(2,128)S(1)} %get-tuple-element.726, ...), kind=kOutput, calls=%fused_computation.12 | convolution fusion | flops 1095761920 | bytes 23364096 | tf_op jit(solution)/shard_map/while/body/eval_jaxpr/while/body/eval_jaxpr/cond/branch_1_fun/qgmk,kgd->qgmd/dot_general | solution.py:43
  218.7 18.0 %conditional.3 = ((f32[2048,1,2]{0,2,1:T(2,128)S(1)}, f32[2048,1,2]{0,2,1:T(2,128)S(1)}, f32[2048,1,2,128]{0,3,2,1:T(8,128)S(1)})) conditional(s32[]{:T(128)} %convert_element_type.42, (f32[2048,1,2]{0,2,1:T(2,128)S(1)}, f32[2048,1,2]{0,2,1:T(2,128)S(1)}, f32[2048,1,2,128]{0,3,2,1:T(8,128)S(1)}) %tuple.146, (s32[]{:T(128)}, s32[]{:T(128)}, s32[]{:T(128)}, ...), branch_computations={%region_2.1_spmd, %region_3.4_spmd} | conditional | flops 2207269888 | bytes 64785456 | solution.py:66
  229.7 7.1 %fusion.12 = f32[2048,1,2,128]{0,3,2,1:T(8,128)S(1)} fusion(f32[1024,2048,2]{1,0,2:T(8,128)S(1)} %get-tuple-element.729, f32[2048,2]{0,1:T(2,128)S(1)} %bitcast.148, pred[2048,1024]{0,1:T(8,128)(4,1)S(1)} %compare_and_fusion, f32[2048,1,2,128]{0,3,2,1:T(8,128)S(1)} %get-tuple-element.261, f32[2048,2]{0,1:T(2,128)S(1)} %get-tuple-element.726, ...), kind=kOutput, calls=%fused_computation.12 | convolution fusion | flops 1095761920 | bytes 23364096 | tf_op jit(solution)/shard_map/while/body/eval_jaxpr/while/body/eval_jaxpr/cond/branch_1_fun/qgmk,kgd->qgmd/dot_general | solution.py:43
  241.9 7.2 %all-to-all-start.1 = ((bf16[8,512,2,128]{3,1,2,0:T(8,128)(2,1)}), bf16[8,512,2,128]{3,1,2,0:T(8,128)(2,1)S(1)}, u32[]{:S(2)}, u32[]{:S(2)}) async-start(bf16[8,512,2,128]{3,1,2,0:T(8,128)(2,1)} %copy.310), calls=%async_computation.1 | async-start | bytes 4194304 | tf_op jit(solution)/shard_map/all_to_all | solution.py:150
  251.4 23.7 %all-to-all-done.1 = bf16[8,512,2,128]{3,1,2,0:T(8,128)(2,1)S(1)} async-done(((bf16[8,512,2,128]{3,1,2,0:T(8,128)(2,1)}), bf16[8,512,2,128]{3,1,2,0:T(8,128)(2,1)S(1)}, u32[]{:S(2)}, u32[]{:S(2)}) %all-to-all-start.1) | async-done | bytes 2097184 | tf_op jit(solution)/shard_map/all_to_all | solution.py:150
  (139 shorter events, 112.0 us)
Async XLA Ops:
  6.5 19.4 %copy-start = (bf16[512,4,128]{2,1,0:T(4,128)(2,1)S(1)}, bf16[512,4,128]{2,1,0:T(4,128)(2,1)}, u32[]{:S(2)}) copy-start(bf16[512,4,128]{2,1,0:T(4,128)(2,1)} %param.13) | copy-start | bytes 1572868
  8.0 18.0 %copy-start.1 = (bf16[512,4,128]{2,1,0:T(4,128)(2,1)S(1)}, bf16[512,4,128]{2,1,0:T(4,128)(2,1)}, u32[]{:S(2)}) copy-start(bf16[512,4,128]{2,1,0:T(4,128)(2,1)} %param.12) | copy-start | bytes 1572868
  19.5 20.3 %all-to-all-start.2 = ((bf16[16,1,2,128,1,128]{5,3,2,4,1,0:T(8,128)(2,1)}), bf16[16,1,2,128,1,128]{5,3,2,4,1,0:T(8,128)(2,1)S(1)}, u32[]{:S(2)}, u32[]{:S(2)}) async-start(bf16[16,1,2,128,1,128]{5,3,2,4,1,0:T(8,128)(2,1)} %bitcast_dynamic-update-slice_fusion), calls=%async_computation.2 | async-start | bytes 2097152 | tf_op jit(solution)/shard_map/all_to_all | solution.py:107
  30.7 15.7 %copy-start.2 = (s32[16]{0:T(128)S(1)}, s32[16]{0:T(128)}, u32[]{:S(2)}) copy-start(s32[16]{0:T(128)} %param.15) | copy-start | bytes 196
  39.8 55.9 %all-to-all-start = ((bf16[512,8,4,128]{3,0,2,1:T(8,128)(2,1)}), bf16[512,8,4,128]{3,0,2,1:T(8,128)(2,1)}, u32[]{:S(2)}, u32[]{:S(2)}) async-start(bf16[512,8,4,128]{3,0,2,1:T(8,128)(2,1)} %pad_maximum_fusion), calls=%async_computation | async-start | bytes 8388608 | tf_op jit(solution)/shard_map/all_to_all | solution.py:14
  95.6 146.3 %all-to-all-start.3 = ((bf16[16,2,1,1,128,128]{5,4,1,3,2,0:T(8,128)(2,1)}), bf16[16,2,1,1,128,128]{5,4,1,3,2,0:T(8,128)(2,1)}, u32[]{:S(2)}, u32[]{:S(2)}) async-start(bf16[16,2,1,1,128,128]{5,4,1,3,2,0:T(8,128)(2,1)} %fusion.28), calls=%async_computation.3 | async-start | bytes 2097152 | tf_op jit(solution)/shard_map/all_to_all | solution.py:112
  241.9 33.2 %all-to-all-start.1 = ((bf16[8,512,2,128]{3,1,2,0:T(8,128)(2,1)}), bf16[8,512,2,128]{3,1,2,0:T(8,128)(2,1)S(1)}, u32[]{:S(2)}, u32[]{:S(2)}) async-start(bf16[8,512,2,128]{3,1,2,0:T(8,128)(2,1)} %copy.310), calls=%async_computation.1 | async-start | bytes 4194304 | tf_op jit(solution)/shard_map/all_to_all | solution.py:150
